TPU v7x, 256 devices: a whole 4x4x8 slice. The times are simulated.
256 devices in a mesh: tm: 64 (over z, y, core), freq: 4 (over x).
Axes of the slice: x: 4, y: 4, z: 8, core: 2. Of those that a mesh axis runs over, the one named last changes fastest.
Arguments:
- snapshots: bfloat16 [4352, 3, 32768], P('tm', None, 'freq'), may hold values from -200 to 200
- block_starts: int32 [32], replicated, may hold values from 0 to 4032, as said below
- freq_index: int32 [16], replicated, may hold values from 0 to 128
Outputs:
- modes: bfloat16 [16, 32, 2, 3, 32768], P(None, None, None, None, ('freq', 'tm'))
- energy: float32 [16], replicated
Inputs may be any that keep to these rules, and one draw needn't show every extreme that they name: `block_starts`: block b starts at b * 128 plus between 0 and 64.
All inputs are finite; a program needn't handle non-finite values.
Results may differ from a plain program's by a relative error of at most 0.0085.
Values may be sent and summed in bfloat16 or wider, within the bound.
A program may use at most 64 MiB of HBM per device.

v0:
```python
import math

import jax
import jax.numpy as jnp
from jax import lax
from jax.sharding import PartitionSpec as P

NB = 32
NFFT = 256
NF = 16
NSIT = 6


def split_up(shard, dim, length):
    before, after = (shard.shape[:dim], shard.shape[dim + 1 :])
    return jnp.moveaxis(shard.reshape(*before, length, -1, *after), dim, 0)


def sent_and_summed(shard, axis, dim):
    blocks = split_up(shard, dim, lax.axis_size(axis))
    arrived = lax.all_to_all(blocks, axis, split_axis=0, concat_axis=0, tiled=True)
    return arrived.sum(axis=0)


def copy_for_each(shard, axis):
    copies = jnp.broadcast_to(shard, (lax.axis_size(axis), *shard.shape))
    return lax.all_to_all(copies, axis, split_axis=0, concat_axis=0, tiled=True)


def over_copies(shard, axis):
    return copy_for_each(shard, axis).sum(axis=0)


def for_sending(shard):
    return jax.tree.map(lambda a: a.astype(jnp.bfloat16) if a.dtype == jnp.float32 else a, shard)


def dft_rows(freq_index):
    times_idx = jnp.arange(NFFT, dtype=jnp.int32)
    phase_int = freq_index[:, None] * times_idx[None, :] % NFFT
    angles = 2.0 * math.pi / NFFT * phase_int.astype(jnp.float32)
    window = 0.5 - 0.5 * jnp.cos(2.0 * math.pi / NFFT * times_idx.astype(jnp.float32))
    scaling = 1.0 / jnp.sqrt(jnp.sum(window * window))
    cosine = window[None, :] * jnp.cos(angles) * scaling
    sine_rows = -window[None, :] * jnp.sin(angles) * scaling
    return jnp.stack([cosine, sine_rows], 1).reshape(2 * NF, NFFT).astype(jnp.bfloat16)


def block_rows(block_starts):
    return block_starts[:, None] + jnp.arange(NFFT, dtype=jnp.int32)[None, :]


def matmul_batch(left, right):
    return jnp.einsum("fij,fjk->fik", left, right, precision=lax.Precision.HIGHEST)


def whiten(summed, points):
    gram_re = summed[:, 0]
    gram_im = summed[:, 1]
    top_rows = jnp.concatenate([gram_re, -gram_im], 2)
    low_rows = jnp.concatenate([gram_im, gram_re], 2)
    hermit = jnp.concatenate([top_rows, low_rows], 1)
    frob = jnp.sqrt(jnp.sum(hermit * hermit, axis=(1, 2)) + 1e-06)
    identity = jnp.eye(2 * NB, dtype=jnp.float32)[None]
    iterate = hermit / frob[:, None, None]
    inverse = jnp.broadcast_to(identity, hermit.shape)
    for iteration in range(NSIT):
        factor = 1.5 * identity - 0.5 * matmul_batch(inverse, iterate)
        iterate = matmul_batch(iterate, factor)
        inverse = matmul_batch(factor, inverse)
    columns = inverse[:, :, :NB] * jnp.sqrt(6.0 * points / frob)[:, None, None]
    upper = columns[:, :NB]
    lower = columns[:, NB:]
    coefficients = jnp.stack([jnp.stack([upper, -lower], 1), jnp.stack([lower, upper], 1)], 1)
    energy = jnp.trace(gram_re, axis1=1, axis2=2) / (3.0 * NB * points)
    return (coefficients, energy)


def local(snapshots, block_starts, freq_index):
    dft_table = dft_rows(freq_index)
    offsets = block_rows(block_starts)
    series = lax.all_to_all(snapshots, "tm", split_axis=2, concat_axis=0, tiled=True)
    count = series.shape[1]
    width = series.shape[2]
    columns_all = series.reshape(series.shape[0], count * width)
    windows = jnp.take(columns_all, offsets, axis=0)
    spectra_part = jnp.einsum(
        "rt,btn->rbn", dft_table, windows, preferred_element_type=jnp.float32
    ).astype(jnp.bfloat16)
    spectra = spectra_part.reshape(2 * NF, NB, count, width)
    width = spectra.shape[3]
    points = float(width * lax.axis_size("tm") * lax.axis_size("freq"))
    flat_spec = spectra.reshape(NF, 2, NB, 3 * width)
    real_part = flat_spec[:, 0]
    imag_part = flat_spec[:, 1]
    gram_re = jnp.einsum("fbn,fcn->fbc", real_part, real_part, preferred_element_type=jnp.float32)
    gram_re = gram_re + jnp.einsum(
        "fbn,fcn->fbc", imag_part, imag_part, preferred_element_type=jnp.float32
    )
    cross_terms = jnp.einsum(
        "fbn,fcn->fbc", real_part, imag_part, preferred_element_type=jnp.float32
    )
    partial_gram = jnp.stack([gram_re, cross_terms - jnp.swapaxes(cross_terms, 1, 2)], 1)
    shared = sent_and_summed(partial_gram, "freq", 0)
    shared = over_copies(shared, "tm")
    coef_part, energy_part = whiten(shared, points)
    coefficients, energy = (
        lax.all_gather(for_sending(coef_part), "freq", axis=0, tiled=True).astype(coef_part.dtype),
        lax.all_gather(for_sending(energy_part), "freq", axis=0, tiled=True).astype(
            energy_part.dtype
        ),
    )
    coef_bf = jnp.transpose(coefficients.astype(jnp.bfloat16), (0, 4, 1, 2, 3))
    modes = jnp.einsum(
        "fjorb,frbn->fjon", coef_bf, flat_spec, preferred_element_type=jnp.float32
    ).astype(jnp.bfloat16)
    return (modes.reshape(NF, NB, 2, 3, width), energy)


def solution(mesh):
    return jax.shard_map(
        local,
        mesh=mesh,
        in_specs=(P("tm", None, "freq"), P(), P()),
        out_specs=(P(None, None, None, None, ("freq", "tm")), P()),
        check_vma=False,
    )
```

profile of v0, /device:TPU:16, one launch (start us, length us, event | category | flops | bytes accessed | tf_op | source)
XLA Modules:
  0.0 322.1 jit_solution(11476231079121534592)
XLA Ops:
  0.6 12.8 %copy.95 = bf16[68,3,8192]{0,1,2:T(4,128)(2,1)} copy(bf16[68,3,8192]{2,0,1:T(8,128)(2,1)} %param.3) | data formatting | bytes 6684672 | tf_op args[0]
  13.4 16.1 %reshape.269 = bf16[64,2,13056]{2,1,0:T(2,128)(2,1)} reshape(bf16[8192,3,68]{2,1,0:T(4,128)(2,1)} %bitcast.101) | data formatting | bytes 6684672
  29.5 12.1 %all-to-all-start = ((bf16[64,2,13056]{2,1,0:T(2,128)(2,1)}), bf16[64,2,13056]{2,1,0:T(2,128)(2,1)S(1)}, u32[]{:S(2)}, u32[]{:S(2)}) async-start(bf16[64,2,13056]{2,1,0:T(2,128)(2,1)} %reshape.269), calls=%async_computation | async-start | bytes 6684672 | tf_op jit(solution)/shard_map/all_to_all | solution.py:82
  41.6 0.6 multiply_reduce_fusion.1
  43.4 76.1 %all-to-all-done = bf16[64,2,13056]{2,1,0:T(2,128)(2,1)S(1)} async-done(((bf16[64,2,13056]{2,1,0:T(2,128)(2,1)}), bf16[64,2,13056]{2,1,0:T(2,128)(2,1)S(1)}, u32[]{:S(2)}, u32[]{:S(2)}) %all-to-all-start) | async-done | bytes 3342368 | tf_op jit(solution)/shard_map/all_to_all | solution.py:82
  119.5 13.4 %reshape.270 = bf16[8192,3,68]{2,1,0:T(4,128)(2,1)} reshape(bf16[64,2,13056]{2,1,0:T(2,128)(2,1)S(1)} %all-to-all-done) | data formatting | bytes 6684672
  132.9 16.7 %copy.96 = bf16[68,3,64,128]{3,1,0,2:T(4,128)(2,1)} copy(bf16[68,3,64,128]{0,1,3,2:T(4,128)(2,1)} %bitcast.100) | data formatting | bytes 6684672 | tf_op jit(solution)/shard_map/all_to_all | solution.py:82
  149.6 2.8 copy.133
  152.5 33.1 %gather_fusion = bf16[8192,384]{1,0:T(8,128)(2,1)} fusion(bf16[4352,384]{1,0:T(8,128)(2,1)S(1)} %bitcast.99, s32[8192]{0:T(1024)S(1)} %broadcast_clamp_fusion), kind=kCustom, calls=%fused_computation | custom fusion | bytes 12615680 | tf_op jit(solution)/shard_map/jit(_take)/gather | solution.py:86
  185.6 4.6 %fusion.4 = bf16[32,32,384]{2,0,1:T(8,128)(2,1)S(1)} fusion(bf16[32,256,1]{1,0,2:T(8,128)(2,1)S(1)} %reshape.265, bf16[32,256,384]{2,1,0:T(8,128)(2,1)} %bitcast.104, pred[32,256]{1,0:T(8,128)(4,1)S(1)} %fusion.29), kind=kOutput, calls=%fused_computation.7 | convolution fusion | flops 204865536 | bytes 7102464 | tf_op jit(solution)/shard_map/rt,btn->rbn/dot_general | solution.py:87
  190.2 0.3 reshape_reshape.3
  190.5 1.1 fusion.40
  191.6 0.3 fusion.16
  191.9 0.5 fusion.15
  192.6 0.3 convolution_add_fusion
  193.3 10.1 %all_to_all.25 = f32[4,1,8192]{2,1,0:T(1,128)S(1)} all-to-all(f32[4,1,8192]{2,1,0:T(1,128)S(1)} %reshape.271), channel_id=1, replica_groups=mesh['tm'=64,'freq'=4] {'freq'}, dimensions={0} | all-to-all | bytes 262144 | tf_op jit(solution)/shard_map/all_to_all | solution.py:21
  203.4 0.5 broadcast.301
  203.9 1.0 reduce
  205.1 4.3 %broadcast_in_dim.41 = f32[64,4,2,32,32]{4,3,2,1,0:T(8,128)} broadcast(f32[4,2,32,32]{3,2,1,0:T(8,128)S(1)} %copy.103), dimensions={1,2,3,4} | broadcast | bytes 2129920 | tf_op jit(solution)/shard_map/broadcast_in_dim | solution.py:26
  209.4 7.8 %reshape.273 = f32[64,1,8192]{2,1,0:T(1,128)} reshape(f32[64,4,2,32,32]{4,3,2,1,0:T(8,128)} %broadcast_in_dim.41) | data formatting | bytes 4194304
  217.2 5.7 %all-to-all-start.2 = ((f32[64,1,8192]{2,1,0:T(1,128)}), f32[64,1,8192]{2,1,0:T(1,128)}, u32[]{:S(2)}, u32[]{:S(2)}) async-start(f32[64,1,8192]{2,1,0:T(1,128)} %reshape.273), calls=%async_computation.2 | async-start | bytes 4194304 | tf_op jit(solution)/shard_map/all_to_all | solution.py:27
  222.9 0.6 dynamic-slice
  224.2 50.0 %all-to-all-done.2 = f32[64,1,8192]{2,1,0:T(1,128)} async-done(((f32[64,1,8192]{2,1,0:T(1,128)}), f32[64,1,8192]{2,1,0:T(1,128)}, u32[]{:S(2)}, u32[]{:S(2)}) %all-to-all-start.2) | async-done | bytes 2097184 | tf_op jit(solution)/shard_map/all_to_all | solution.py:27
  274.1 7.5 %reduce.1 = f32[64,8192]{1,0:T(8,128)S(1)} reduce(f32[64,1,8192]{2,1,0:T(1,128)} %all-to-all-done.2, f32[]{:T(128)} %broadcast.301), dimensions={1}, to_apply=%all_to_all.21.reduce_sub_computation | reduce | bytes 4194308 | tf_op jit(solution)/shard_map/all_to_all | solution.py:27
  281.7 4.8 %reshape.274 = f32[64,4,2,32,32]{4,3,2,1,0:T(8,128)} reshape(f32[64,8192]{1,0:T(8,128)S(1)} %reduce.1) | data formatting | bytes 4194304
  286.5 4.4 %reduce_sum.48 = f32[4,2,32,32]{3,2,1,0:T(8,128)S(1)} reduce(f32[64,4,2,32,32]{4,3,2,1,0:T(8,128)} %reshape.274, f32[]{:T(128)} %constant.22.clone.1), dimensions={0}, to_apply=%region_2.3 | reduce | flops 516096 | bytes 2129924 | tf_op jit(solution)/shard_map/reduce_sum | solution.py:31
  291.2 0.4 fusion.12
  291.6 0.3 fusion.39
  292.2 0.3 fusion.11
  292.4 0.3 fusion.43
  292.7 0.3 fusion.42
  293.0 0.3 fusion.10
  293.2 0.3 fusion.45
  293.5 0.3 fusion.44
  293.8 0.3 fusion.9
  294.0 0.3 fusion.47
  294.3 0.3 fusion.46
  294.5 0.3 fusion.8
  294.8 0.3 fusion.49
  295.1 0.3 fusion.48
  295.3 0.3 fusion.7
  295.6 0.4 convolution_multiply_fusion.6
  296.2 12.9 %all_gather.6 = bf16[16,2,2,32,32]{3,4,0,2,1:T(8,128)(2,1)S(1)} all-gather(bf16[4,2,2,32,32]{3,4,0,2,1:T(8,128)(2,1)S(1)} %pad_maximum_fusion.1), channel_id=1, replica_groups=mesh['tm'=64,'freq'=4] {'freq'}, dimensions={0}, use_global_device_ids=true | all-gather | bytes 163840 | tf_op jit(solution)/shard_map/all_gather | solution.py:108
  309.2 0.4 bitcast_convert_fusion
  309.6 0.3 reshape.249
  310.1 2.1 copy.109
  312.2 9.4 %all-reduce = bf16[16]{0:T(256)(128)(2,1)S(1)} all-reduce(bf16[16]{0:T(256)(128)(2,1)S(1)} %dynamic-update-slice), channel_id=1, replica_groups=mesh['tm'=64,'freq'=4] {'freq'}, use_global_device_ids=true, to_apply=%add | all-reduce | flops 16 | bytes 64
  321.6 0.5 convert_element_type.64
  (37 shorter events, 2.2 us)
Async XLA Ops:
  13.4 29.6 %copy-start.1 = (s32[16]{0:T(128)S(1)}, s32[16]{0:T(128)}, u32[]{:S(2)}) copy-start(s32[16]{0:T(128)} %param.5) | copy-start | bytes 196
  29.4 13.7 %copy-start = (s32[32]{0:T(128)S(1)}, s32[32]{0:T(128)}, u32[]{:S(2)}) copy-start(s32[32]{0:T(128)} %param.4) | copy-start | bytes 388
  29.5 90.1 %all-to-all-start = ((bf16[64,2,13056]{2,1,0:T(2,128)(2,1)}), bf16[64,2,13056]{2,1,0:T(2,128)(2,1)S(1)}, u32[]{:S(2)}, u32[]{:S(2)}) async-start(bf16[64,2,13056]{2,1,0:T(2,128)(2,1)} %reshape.269), calls=%async_computation | async-start | bytes 6684672 | tf_op jit(solution)/shard_map/all_to_all | solution.py:82
  209.4 13.5 %copy-start.2 = (u32[256]{0:T(256)S(1)}, u32[256]{0:T(256)}, u32[]{:S(2)}) copy-start(u32[256]{0:T(256)} %constant.56) | copy-start | bytes 3076
  217.2 57.0 %all-to-all-start.2 = ((f32[64,1,8192]{2,1,0:T(1,128)}), f32[64,1,8192]{2,1,0:T(1,128)}, u32[]{:S(2)}, u32[]{:S(2)}) async-start(f32[64,1,8192]{2,1,0:T(1,128)} %reshape.273), calls=%async_computation.2 | async-start | bytes 4194304 | tf_op jit(solution)/shard_map/all_to_all | solution.py:27
where the time goes:
time: 324 us; the launch traced here: 322 us
  waiting for transfers between devices  126 us (39%)
  local copies, waits for them, and re-layouts  118 us (36%)
  blocking collectives  32.4 us (10%)
  starting transfers between devices  17.8 us (5%)
  other arithmetic  15.1 us (5%)
  matrix products  10.8 us (3%)
    all_to_all x1, waiting for transfers between devices, local(): lax.all_to_all(snapshots, 'tm', split_axis=2, concat_axis=0, tiled=True)  76.1 us
    unnamed x19, local copies, waits for them, and re-layouts  61 us
    all_to_all x1, waiting for transfers between devices, copy_for_each(): return lax.all_to_all(copies, axis, split_axis=0, concat_axis=0, tiled=True)  50 us
    gather x1, local copies, waits for them, and re-layouts, local(): windows = jnp.take(columns_all, offsets, axis=0)  33.1 us
    all_to_all x1, local copies, waits for them, and re-layouts, local(): lax.all_to_all(snapshots, 'tm', split_axis=2, concat_axis=0, tiled=True)  16.7 us
    all_gather x1, blocking collectives, local(): lax.all_gather(for_sending(coef_part), 'freq', axis=0, tiled=True)  12.9 us
    all_to_all x1, starting transfers between devices, local(): lax.all_to_all(snapshots, 'tm', split_axis=2, concat_axis=0, tiled=True)  12.1 us
    all_to_all x1, blocking collectives, sent_and_summed(): lax.all_to_all(blocks, axis, split_axis=0, concat_axis=0, tiled=True)  10.1 us
  transfers between devices with their start and end apart: 2, of which 2 were waited for; matrix products, arithmetic and copies ran while one was open for 1% of the time, Pallas kernels for 0%

commit v1 on v0

v1 whole, which is shorter than its diff:
```python
import functools
import math

import jax
import jax.numpy as jnp
from jax import lax
from jax.experimental import pallas as pl
from jax.experimental.pallas import tpu as pltpu
from jax.sharding import PartitionSpec as P

NB = 32
NFFT = 256
NF = 16
NSIT = 6
SLABS = 8
PEERS = 8
ROWS = 68
OWN = 4
WB = 8
LANES = 128
POINTS = 32768.0
MESH = pl.DeviceIdType.MESH


def dft_rows(freq_index):
    times_idx = jnp.arange(NFFT, dtype=jnp.int32)
    phase_int = freq_index[:, None] * times_idx[None, :] % NFFT
    angles = 2.0 * math.pi / NFFT * phase_int.astype(jnp.float32)
    window = 0.5 - 0.5 * jnp.cos(2.0 * math.pi / NFFT * times_idx.astype(jnp.float32))
    scaling = 1.0 / jnp.sqrt(jnp.sum(window * window))
    cosine = window[None, :] * jnp.cos(angles) * scaling
    sine_rows = -window[None, :] * jnp.sin(angles) * scaling
    return jnp.stack([cosine, sine_rows], 1).reshape(2 * NF, NFFT).astype(jnp.bfloat16)


def one_hot_rows(rows, cols, source):
    i = lax.broadcasted_iota(jnp.int32, (rows, cols), 0)
    j = lax.broadcasted_iota(jnp.int32, (rows, cols), 1)
    return jnp.where(source(i) == j, 1.0, 0.0).astype(jnp.bfloat16)


def dot_nn(a, b, precision=None):
    return lax.dot_general(
        a, b, (((1,), (0,)), ((), ())), precision=precision, preferred_element_type=jnp.float32
    )


def dot_nt(a, b, precision=None):
    return lax.dot_general(
        a, b, (((1,), (1,)), ((), ())), precision=precision, preferred_element_type=jnp.float32
    )


def step_slab(step):
    return lax.rem(step, 2) * 4 + lax.rem(step // 2, 2) * 2 + step // 4


def kernel(
    xt,
    table,
    starts,
    out,
    energy_out,
    weights,
    rbuf,
    own,
    hsend,
    hrecv,
    zsend,
    spec,
    sxy,
    gsend,
    grecv,
    bsend,
    brecv,
    csend,
    crecv,
    ysend_sem,
    yrecv_sem,
    hsend_sem,
    hrecv_sem,
    zsend_sem,
    zrecv_sem,
    gsend_sem,
    grecv_sem,
    bsend_sem,
    brecv_sem,
    csend_sem,
    crecv_sem,
):
    tm = lax.axis_index("tm")
    fx = lax.axis_index("freq")
    z = tm // PEERS
    me = lax.rem(tm, PEERS)
    y = me // 2
    core = lax.rem(me, 2)

    def slab_peer(p):
        return {"tm": z * PEERS + p, "freq": fx}

    def column_peer(zz):
        return {"tm": zz * PEERS + me, "freq": fx}

    def plane_peer(k):
        return {"tm": z * PEERS + lax.rem(k, 4) * 2 + core, "freq": k // 4}

    def line_peer(k):
        return {"tm": (k // 2) * PEERS + y * 2 + lax.rem(k, 2), "freq": fx}

    plane_me = fx * 4 + y
    line_me = z * 2 + core

    hrecv[...] = jnp.zeros_like(hrecv)

    barrier = pltpu.get_barrier_semaphore()

    def greet(device):
        pl.semaphore_signal(barrier, inc=1, device_id=device, device_id_type=MESH)

    @pl.loop(1, PEERS)
    def _(d):
        greet(slab_peer(lax.rem(me + d, PEERS)))

    @pl.loop(1, 16)
    def _(d):
        greet(plane_peer(lax.rem(plane_me + d, 16)))
        greet(line_peer(lax.rem(line_me + d, 16)))

    pl.semaphore_wait(barrier, 37)

    def y_copy(zz, p):
        cols = pl.ds(pl.multiple_of((zz * PEERS + p) * LANES, LANES), LANES)
        return pltpu.make_async_remote_copy(
            src_ref=xt.at[:, :, cols],
            dst_ref=rbuf.at[zz, me],
            send_sem=ysend_sem.at[zz, p],
            recv_sem=yrecv_sem.at[zz, me],
            device_id=slab_peer(p),
            device_id_type=MESH,
        )

    def y_local(zz):
        cols = pl.ds(pl.multiple_of((zz * PEERS + me) * LANES, LANES), LANES)
        return pltpu.make_async_copy(xt.at[:, :, cols], rbuf.at[zz, me], yrecv_sem.at[zz, me])

    @pl.loop(0, SLABS)
    def _(s):
        zz = step_slab(s)
        y_local(zz).start()

        @pl.loop(1, PEERS)
        def _(d):
            y_copy(zz, lax.rem(me + d, PEERS)).start()

    tau = lax.broadcasted_iota(jnp.int32, (NFFT, ROWS), 0)
    tt = lax.broadcasted_iota(jnp.int32, (NFFT, ROWS), 1)
    for i in range(WB):
        b = z * OWN - 2 + i
        first = starts[jnp.clip(b, 0, NB - 1)]
        for src in range(PEERS):
            origin = z * (PEERS * ROWS) + src * ROWS
            pick = jnp.where(tau + first == tt + origin, 1.0, 0.0).astype(jnp.bfloat16)
            weights[src, pl.ds(i * 32, 32), :] = dot_nn(table[...], pick).astype(jnp.bfloat16)

    order = one_hot_rows(128, 128, lambda i: lax.rem(i // 2, 4) * 32 + (i // 8) * 2 + lax.rem(i, 2))

    def h_copy(zz, slot, target):
        return pltpu.make_async_remote_copy(
            src_ref=hsend.at[zz, slot],
            dst_ref=hrecv.at[zz, slot],
            send_sem=hsend_sem.at[zz, slot],
            recv_sem=hrecv_sem.at[zz, slot],
            device_id=column_peer(target),
            device_id_type=MESH,
        )

    def helpers(zz, act_send, act_recv):
        up = jnp.minimum(z + 1, SLABS - 1)
        down = jnp.maximum(z - 1, 0)
        for slot, target, sends, takes in (
            (0, up, z <= 6, z >= 1),
            (1, up, (z >= 4) & (z <= 6), z >= 5),
            (2, down, z == 1, z == 0),
            (3, down, (z >= 1) & (z <= 5), z <= 4),
        ):
            if act_send is not None:

                @pl.when(sends)
                def _():
                    act_send(h_copy(zz, slot, target))

            if act_recv is not None:

                @pl.when(takes)
                def _():
                    act_recv(h_copy(zz, slot, target))

    def z_copy(zz, target):
        return pltpu.make_async_remote_copy(
            src_ref=zsend.at[zz],
            dst_ref=spec.at[z],
            send_sem=zsend_sem.at[zz],
            recv_sem=zrecv_sem.at[z],
            device_id=column_peer(target),
            device_id_type=MESH,
        )

    def partial(s):
        zz = step_slab(s)
        y_local(zz).wait()

        @pl.loop(1, PEERS)
        def _(d):
            p = lax.rem(me + d, PEERS)
            pltpu.make_async_remote_copy(
                src_ref=rbuf.at[zz, p],
                dst_ref=rbuf.at[zz, p],
                send_sem=ysend_sem.at[zz, p],
                recv_sem=yrecv_sem.at[zz, p],
                device_id=slab_peer(p),
                device_id_type=MESH,
            ).wait_recv()

        for c in range(3):
            acc = dot_nn(weights[0], rbuf[zz, 0, c])
            for src in range(1, PEERS):
                acc = acc + dot_nn(weights[src], rbuf[zz, src, c])
            cols = pl.ds(c * LANES, LANES)
            acc = acc.reshape(WB, 32, LANES)
            hsend[zz, 2:4, :, cols] = acc[0:2]
            own[lax.rem(s, 2), :, :, cols] = acc[2:6]
            hsend[zz, 0:2, :, cols] = acc[6:8]
        helpers(zz, lambda copy: copy.start(), None)

    def finish(s):
        zz = step_slab(s)
        helpers(zz, None, lambda copy: copy.wait_recv())
        total = (own[lax.rem(s, 2)] + hrecv[zz]).astype(jnp.bfloat16).reshape(OWN * 32, 3 * LANES)
        rows = dot_nn(order, total).astype(jnp.bfloat16)
        for c in range(3):
            zsend[zz, c] = rows[:, c * LANES : (c + 1) * LANES]

        @pl.when(zz == z)
        def _():
            pltpu.make_async_copy(zsend.at[zz], spec.at[z], zrecv_sem.at[z]).start()

        @pl.when(zz != z)
        def _():
            z_copy(zz, zz).start()

    partial(0)

    @pl.loop(1, SLABS)
    def _(s):
        partial(s)
        finish(s - 1)

    finish(SLABS - 1)

    pltpu.make_async_copy(zsend.at[z], spec.at[z], zrecv_sem.at[z]).wait()

    @pl.loop(1, SLABS)
    def _(d):
        zz = lax.rem(z + d, SLABS)
        pltpu.make_async_remote_copy(
            src_ref=spec.at[zz],
            dst_ref=spec.at[zz],
            send_sem=zsend_sem.at[zz],
            recv_sem=zrecv_sem.at[zz],
            device_id=column_peer(zz),
            device_id_type=MESH,
        ).wait_recv()

    arrange = one_hot_rows(
        128,
        128,
        lambda i: (lax.rem(i, 32) // 4) * 16
        + (i // 64) * 8
        + lax.rem(i, 4) * 2
        + lax.rem(i // 32, 2),
    )
    for pair in range(NF // 2):
        grams = [None, None]
        for c in range(3):
            stacked = spec[:, c, pl.ds(pair * 16, 16), :].reshape(128, LANES)
            placed = dot_nn(arrange, stacked).astype(jnp.bfloat16)
            sxy[pair, c] = placed
            for h in range(2):
                xr = placed[h * 64 : h * 64 + 32]
                yr = placed[h * 64 + 32 : h * 64 + 64]
                left = jnp.concatenate([xr, -yr], 0)
                right = jnp.concatenate([yr, xr], 0)
                term = dot_nt(left, xr) + dot_nt(right, yr)
                grams[h] = term if c == 0 else grams[h] + term
        for h in range(2):
            g = grams[h]
            gsend[pair * 2 + h] = jnp.concatenate([g[16 * k : 16 * k + 16] for k in range(4)], 1)

    def g_copy(k):
        return pltpu.make_async_remote_copy(
            src_ref=gsend.at[k],
            dst_ref=grecv.at[plane_me],
            send_sem=gsend_sem.at[k],
            recv_sem=grecv_sem.at[plane_me],
            device_id=plane_peer(k),
            device_id_type=MESH,
        )

    @pl.loop(1, 16)
    def _(d):
        g_copy(lax.rem(plane_me + d, 16)).start()

    grecv[plane_me] = gsend[plane_me]

    @pl.loop(1, 16)
    def _(d):
        k = lax.rem(plane_me + d, 16)
        pltpu.make_async_remote_copy(
            src_ref=grecv.at[k],
            dst_ref=grecv.at[k],
            send_sem=gsend_sem.at[k],
            recv_sem=grecv_sem.at[k],
            device_id=plane_peer(k),
            device_id_type=MESH,
        ).wait_recv()

    bsend[...] = jnp.sum(grecv[...], axis=0)

    @pl.loop(1, 16)
    def _(d):
        k = lax.rem(line_me + d, 16)
        pltpu.make_async_remote_copy(
            src_ref=bsend,
            dst_ref=brecv.at[line_me],
            send_sem=bsend_sem.at[k],
            recv_sem=brecv_sem.at[line_me],
            device_id=line_peer(k),
            device_id_type=MESH,
        ).start()

    brecv[line_me] = bsend[...]

    @pl.loop(1, 16)
    def _(d):
        k = lax.rem(line_me + d, 16)
        pltpu.make_async_remote_copy(
            src_ref=brecv.at[k],
            dst_ref=brecv.at[k],
            send_sem=bsend_sem.at[k],
            recv_sem=brecv_sem.at[k],
            device_id=line_peer(k),
            device_id_type=MESH,
        ).wait_recv()

    packed = jnp.sum(brecv[...], axis=0)
    gram = jnp.concatenate([packed[:, 32 * k : 32 * k + 32] for k in range(4)], 0)
    gram_re, gram_im = gram[:NB], gram[NB:]
    hermit = jnp.concatenate(
        [jnp.concatenate([gram_re, -gram_im], 1), jnp.concatenate([gram_im, gram_re], 1)], 0
    )
    eye = jnp.where(
        lax.broadcasted_iota(jnp.int32, (64, 64), 0) == lax.broadcasted_iota(jnp.int32, (64, 64), 1),
        1.0,
        0.0,
    )
    square = jnp.sum(jnp.sum(hermit * hermit, axis=1, keepdims=True), axis=0, keepdims=True)
    frob = jnp.sqrt(square + 1e-06)
    trace = jnp.sum(jnp.sum(gram_re * eye[:NB, :NB], axis=1, keepdims=True), axis=0, keepdims=True)
    energy = jnp.broadcast_to(trace / (3.0 * NB * POINTS), (16, LANES))
    iterate = hermit / frob
    inverse = eye
    high = lax.Precision.HIGHEST
    for iteration in range(NSIT):
        if iteration == 0:
            factor = 1.5 * eye - 0.5 * iterate
            inverse = factor
        else:
            factor = 1.5 * eye - 0.5 * dot_nn(inverse, iterate, high)
            inverse = dot_nn(factor, inverse, high)
        if iteration < NSIT - 1:
            iterate = dot_nn(iterate, factor, high)
    columns = inverse[:, :NB] * jnp.sqrt(6.0 * POINTS / frob)
    upper, lower = columns[:NB], columns[NB:]
    coef = jnp.concatenate(
        [jnp.concatenate([upper, lower], 1), jnp.concatenate([-lower, upper], 1)], 0
    ).astype(jnp.bfloat16)
    high_part = energy.astype(jnp.bfloat16)
    rest = energy - high_part.astype(jnp.float32)
    mid_part = rest.astype(jnp.bfloat16)
    low_part = (rest - mid_part.astype(jnp.float32)).astype(jnp.bfloat16)
    csend[0:32, :] = jnp.concatenate([coef[:NB], coef[NB:]], 1)
    csend[32:48, :] = high_part
    csend[48:64, :] = mid_part
    csend[64:80, :] = low_part

    @pl.loop(1, 16)
    def _(d):
        k = lax.rem(plane_me + d, 16)
        pltpu.make_async_remote_copy(
            src_ref=csend,
            dst_ref=crecv.at[plane_me],
            send_sem=csend_sem.at[k],
            recv_sem=crecv_sem.at[plane_me],
            device_id=plane_peer(k),
            device_id_type=MESH,
        ).start()

    crecv[plane_me] = csend[...]

    @pl.loop(1, 16)
    def _(d):
        k = lax.rem(plane_me + d, 16)
        pltpu.make_async_remote_copy(
            src_ref=crecv.at[k],
            dst_ref=crecv.at[k],
            send_sem=csend_sem.at[k],
            recv_sem=crecv_sem.at[k],
            device_id=plane_peer(k),
            device_id_type=MESH,
        ).wait_recv()

    pick_row = one_hot_rows(192, 64, lambda i: lax.rem(i, 2) * 32 + i // 6)
    row_c = lax.rem(lax.broadcasted_iota(jnp.int32, (192, 192), 0) // 2, 3)
    col_c = lax.broadcasted_iota(jnp.int32, (192, 192), 1) // 64
    same_c = row_c == col_c
    for f in range(NF):
        message = crecv[f]
        coef_f = jnp.concatenate([message[0:32, 0:64], message[0:32, 64:128]], 0)
        wide = lax.dot_general(
            pick_row, coef_f, (((1,), (1,)), ((), ())), preferred_element_type=jnp.float32
        )
        wide = jnp.where(same_c, jnp.concatenate([wide, wide, wide], 1), 0.0).astype(jnp.bfloat16)
        stacked = jnp.concatenate(
            [sxy[f // 2, c, pl.ds((f % 2) * 64, 64), :] for c in range(3)], 0
        )
        out[pl.ds(f * 192, 192), :] = dot_nn(wide, stacked).astype(jnp.bfloat16)
        energy_out[pl.ds(f, 1), :] = (
            message[32:48].astype(jnp.float32)
            + message[48:64].astype(jnp.float32)
            + message[64:80].astype(jnp.float32)
        )[0:1]

    @pl.loop(0, SLABS)
    def _(s):
        @pl.loop(1, PEERS)
        def _(d):
            y_copy(s, lax.rem(me + d, PEERS)).wait_send()

        helpers(s, lambda copy: copy.wait_send(), None)

        @pl.when(s != z)
        def _():
            z_copy(s, s).wait_send()

    @pl.loop(1, 16)
    def _(d):
        k = lax.rem(plane_me + d, 16)
        g_copy(k).wait_send()
        pltpu.make_async_remote_copy(
            src_ref=csend,
            dst_ref=crecv.at[plane_me],
            send_sem=csend_sem.at[k],
            recv_sem=crecv_sem.at[plane_me],
            device_id=plane_peer(k),
            device_id_type=MESH,
        ).wait_send()
        q = lax.rem(line_me + d, 16)
        pltpu.make_async_remote_copy(
            src_ref=bsend,
            dst_ref=brecv.at[line_me],
            send_sem=bsend_sem.at[q],
            recv_sem=brecv_sem.at[line_me],
            device_id=line_peer(q),
            device_id_type=MESH,
        ).wait_send()


def local(snapshots, block_starts, freq_index):
    xt = jnp.transpose(snapshots, (1, 0, 2))
    table = dft_rows(freq_index)
    dma = pltpu.SemaphoreType.DMA
    vmem = pltpu.VMEM
    bf, f32 = jnp.bfloat16, jnp.float32
    modes, energy = pl.pallas_call(
        kernel,
        out_shape=(
            jax.ShapeDtypeStruct((NF * 192, LANES), bf),
            jax.ShapeDtypeStruct((NF, LANES), f32),
        ),
        in_specs=[
            pl.BlockSpec(memory_space=pl.ANY),
            pl.BlockSpec(memory_space=pltpu.VMEM),
            pl.BlockSpec(memory_space=pltpu.SMEM),
        ],
        out_specs=(
            pl.BlockSpec(memory_space=pltpu.VMEM),
            pl.BlockSpec(memory_space=pltpu.VMEM),
        ),
        scratch_shapes=[
            vmem((PEERS, WB * 32, ROWS), bf),
            vmem((SLABS, PEERS, 3, ROWS, LANES), bf),
            vmem((2, OWN, 32, 3 * LANES), f32),
            vmem((SLABS, 4, 32, 3 * LANES), f32),
            vmem((SLABS, 4, 32, 3 * LANES), f32),
            vmem((SLABS, 3, 128, LANES), bf),
            vmem((SLABS, 3, 128, LANES), bf),
            vmem((NF // 2, 3, 128, LANES), bf),
            vmem((NF, 16, LANES), f32),
            vmem((NF, 16, LANES), f32),
            vmem((16, LANES), f32),
            vmem((16, 16, LANES), f32),
            vmem((80, LANES), bf),
            vmem((16, 80, LANES), bf),
            dma((SLABS, PEERS)),
            dma((SLABS, PEERS)),
            dma((SLABS, 4)),
            dma((SLABS, 4)),
            dma((SLABS,)),
            dma((SLABS,)),
            dma((16,)),
            dma((16,)),
            dma((16,)),
            dma((16,)),
            dma((16,)),
            dma((16,)),
        ],
        compiler_params=pltpu.CompilerParams(collective_id=0, has_side_effects=True),
        name="modes",
    )(xt, table, block_starts)
    modes = modes.reshape(NF, NB, 3, 2, LANES)
    return (jnp.transpose(modes, (0, 1, 3, 2, 4)), energy[:, 0])


def solution(mesh):
    return jax.shard_map(
        local,
        mesh=mesh,
        in_specs=(P("tm", None, "freq"), P(), P()),
        out_specs=(P(None, None, None, None, ("freq", "tm")), P()),
        check_vma=False,
    )
```

time: 324 us -> 106 us (0.33)
  the two profiles are of different devices: /device:TPU:16 before, /device:TPU:1 now
where the time goes in v1:
time: 106 us
  Pallas kernels  98.6 us (93%)
  local copies, waits for them, and re-layouts  4.55 us (4%)
  other arithmetic  1.51 us (1%)
  between operations  1.34 us (1%)
    pallas_call x1, Pallas kernels, local(): pl.pallas_call(kernel, out_shape=(jax.ShapeDtypeStruct((NF * 192, LANES),...  98.6 us
    unnamed x1, local copies, waits for them, and re-layouts  2.59 us

profile of v1, /device:TPU:1, one launch (start us, length us, event | category | flops | bytes accessed | tf_op | source)
XLA Modules:
  0.0 106.0 jit_solution(18213621201892772162)
XLA Ops:
  0.6 0.6 multiply_reduce_fusion
  2.0 0.8 multiply_convert_fusion.1
  2.9 0.6 convert_element_type.33.table
  3.5 98.6 %modes.1 = (bf16[3072,128]{1,0:T(8,128)(2,1)}, f32[16,128]{1,0:T(8,128)}) custom-call(bf16[3,68,8192]{2,1,0:T(8,128)(2,1)} %bitcast.4, bf16[32,256]{1,0:T(8,128)(2,1)} %convert_element_type.33.table, s32[32]{0:T(128)} %starts.1), custom_call_target="tpu_custom_call" | custom-call | tf_op jit(solution)/shard_map/modes/pallas_call | solution.py:484
  102.1 1.3 %slice_reduce_fusion = f32[16]{0:T(128)} fusion(f32[16,128]{1,0:T(8,128)} %get-tuple-element.5), kind=kLoop, calls=%fused_computation.12 | loop fusion | bytes 128 | tf_op jit(solution)/shard_map/slice | solution.py:531
  103.4 2.6 %copy.7 = bf16[16,32,2,3,128]{4,2,3,1,0:T(2,128)(2,1)} copy(bf16[16,32,2,3,128]{4,2,3,1,0:T(2,128)(2,1)} %bitcast.5) | data formatting | bytes 1572864
  (3 shorter events, 0.1 us)

commit v2 on v1

v2 whole, which is shorter than its diff:
```python
import functools
import math

import jax
import jax.numpy as jnp
from jax import lax
from jax.experimental import pallas as pl
from jax.experimental.pallas import tpu as pltpu
from jax.sharding import PartitionSpec as P

NB = 32
NFFT = 256
NF = 16
NSIT = 6
SLABS = 8
PEERS = 8
ROWS = 68
OWN = 4
WB = 8
UNITS = 3 * SLABS
AHEAD = 6
LAG = 3
STEP = 16
LANES = 128
POINTS = 32768.0
MESH = pl.DeviceIdType.MESH


def dft_rows(freq):
    row = lax.broadcasted_iota(jnp.int32, (2 * NF, NFFT), 0)
    time = lax.broadcasted_iota(jnp.int32, (2 * NF, NFFT), 1)
    bins = jnp.zeros((2 * NF, NFFT), jnp.int32)
    for f in range(NF):
        bins = jnp.where(row // 2 == f, freq[f], bins)
    angles = 2.0 * math.pi / NFFT * lax.rem(bins * time, NFFT).astype(jnp.float32)
    window = 0.5 - 0.5 * jnp.cos(2.0 * math.pi / NFFT * time[0:8].astype(jnp.float32))
    scaling = 1.0 / jnp.sqrt(jnp.sum((window * window)[0:1], axis=1, keepdims=True))
    window = jnp.concatenate([window] * (2 * NF // 8), 0)
    wave = jnp.where(lax.rem(row, 2) == 0, window * jnp.cos(angles), -window * jnp.sin(angles))
    return (wave * scaling).astype(jnp.bfloat16)


def one_hot_rows(rows, cols, source):
    i = lax.broadcasted_iota(jnp.int32, (rows, cols), 0)
    j = lax.broadcasted_iota(jnp.int32, (rows, cols), 1)
    return jnp.where(source(i) == j, 1.0, 0.0).astype(jnp.bfloat16)


def dot_nn(a, b, precision=None):
    return lax.dot_general(
        a, b, (((1,), (0,)), ((), ())), precision=precision, preferred_element_type=jnp.float32
    )


def dot_nt(a, b, precision=None):
    return lax.dot_general(
        a, b, (((1,), (1,)), ((), ())), precision=precision, preferred_element_type=jnp.float32
    )


def step_slab(step):
    return lax.rem(step, 2) * 4 + lax.rem(step // 2, 2) * 2 + step // 4


def kernel(
    xt,
    starts_hbm,
    freq_hbm,
    sxy,
    coef_out,
    starts,
    freq,
    weights,
    rbuf,
    own,
    hsend,
    hrecv,
    zsend,
    spec,
    gacc,
    gsend,
    grecv,
    bsend,
    brecv,
    csend,
    crecv,
    ysend_sem,
    yrecv_sem,
    hsend_sem,
    hrecv_sem,
    zsend_sem,
    zrecv_sem,
    gsend_sem,
    grecv_sem,
    bsend_sem,
    brecv_sem,
    csend_sem,
    crecv_sem,
    small_sem,
):
    tm = lax.axis_index("tm")
    fx = lax.axis_index("freq")
    z = tm // PEERS
    me = lax.rem(tm, PEERS)
    y = me // 2
    core = lax.rem(me, 2)

    def slab_peer(p):
        return {"tm": z * PEERS + p, "freq": fx}

    def column_peer(zz):
        return {"tm": zz * PEERS + me, "freq": fx}

    def plane_peer(k):
        return {"tm": z * PEERS + lax.rem(k, 4) * 2 + core, "freq": k // 4}

    def line_peer(k):
        return {"tm": (k // 2) * PEERS + y * 2 + lax.rem(k, 2), "freq": fx}

    plane_me = fx * 4 + y
    line_me = z * 2 + core

    starts_copy = pltpu.make_async_copy(starts_hbm, starts, small_sem.at[0])
    freq_copy = pltpu.make_async_copy(freq_hbm, freq, small_sem.at[1])
    starts_copy.start()
    freq_copy.start()

    barrier = pltpu.get_barrier_semaphore()

    def greet(device):
        pl.semaphore_signal(barrier, inc=1, device_id=device, device_id_type=MESH)

    @pl.loop(1, PEERS)
    def _(d):
        greet(slab_peer(lax.rem(me + d, PEERS)))

    @pl.loop(1, 16)
    def _(d):
        greet(plane_peer(lax.rem(plane_me + d, 16)))
        greet(line_peer(lax.rem(line_me + d, 16)))

    starts_copy.wait()
    freq_copy.wait()
    table = dft_rows(freq)
    pl.semaphore_wait(barrier, 37)

    def y_copy(c, zz, p):
        cols = pl.ds(pl.multiple_of((zz * PEERS + p) * LANES, LANES), LANES)
        return pltpu.make_async_remote_copy(
            src_ref=xt.at[c, :, cols],
            dst_ref=rbuf.at[c, zz, me],
            send_sem=ysend_sem.at[c, zz, p],
            recv_sem=yrecv_sem.at[c, zz, me],
            device_id=slab_peer(p),
            device_id_type=MESH,
        )

    def y_arrival(c, zz, p):
        return pltpu.make_async_remote_copy(
            src_ref=rbuf.at[c, zz, p],
            dst_ref=rbuf.at[c, zz, p],
            send_sem=ysend_sem.at[c, zz, p],
            recv_sem=yrecv_sem.at[c, zz, p],
            device_id=slab_peer(p),
            device_id_type=MESH,
        )

    def y_local(c, zz):
        cols = pl.ds(pl.multiple_of((zz * PEERS + me) * LANES, LANES), LANES)
        return pltpu.make_async_copy(
            xt.at[c, :, cols], rbuf.at[c, zz, me], yrecv_sem.at[c, zz, me]
        )

    def y_start(u):
        c, zz = u // SLABS, step_slab(lax.rem(u, SLABS))

        @pl.loop(1, PEERS)
        def _(d):
            y_copy(c, zz, lax.rem(me + d, PEERS)).start()

        y_local(c, zz).start()

    @pl.loop(0, AHEAD)
    def _(u):
        y_start(u)

    tau = lax.broadcasted_iota(jnp.int32, (NFFT, ROWS), 0)
    tt = lax.broadcasted_iota(jnp.int32, (NFFT, ROWS), 1)
    lag = tau - tt
    for i in range(WB):
        b = z * OWN - 2 + i
        first = starts[jnp.clip(b, 0, NB - 1)]
        for src in range(PEERS):
            origin = z * (PEERS * ROWS) + src * ROWS
            pick = jnp.where(lag == origin - first, 1.0, 0.0).astype(jnp.bfloat16)
            weights[src, pl.ds(i * 32, 32), :] = dot_nn(table, pick).astype(jnp.bfloat16)

    order = one_hot_rows(128, 128, lambda i: lax.rem(i // 2, 4) * 32 + (i // 8) * 2 + lax.rem(i, 2))
    arrange = one_hot_rows(
        128,
        128,
        lambda i: (lax.rem(i, 32) // 4) * 16
        + (i // 64) * 8
        + lax.rem(i, 4) * 2
        + lax.rem(i // 32, 2),
    )

    def h_copy(c, zz, slot, target):
        return pltpu.make_async_remote_copy(
            src_ref=hsend.at[c, zz, slot],
            dst_ref=hrecv.at[c, zz, slot],
            send_sem=hsend_sem.at[c, zz, slot],
            recv_sem=hrecv_sem.at[c, zz, slot],
            device_id=column_peer(target),
            device_id_type=MESH,
        )

    def helpers(c, zz, act_send=None, act_take=None):
        up = jnp.minimum(z + 1, SLABS - 1)
        down = jnp.maximum(z - 1, 0)
        for slot, target, sends, takes in (
            (0, up, z <= 6, z >= 1),
            (1, up, (z >= 4) & (z <= 6), z >= 5),
            (2, down, z == 1, z == 0),
            (3, down, (z >= 1) & (z <= 5), z <= 4),
        ):
            if act_send is not None:

                @pl.when(sends)
                def _():
                    act_send(h_copy(c, zz, slot, target))

            if act_take is not None:

                @pl.when(takes)
                def _():
                    act_take(h_copy(c, zz, slot, target), slot)

    def z_copy(c, zz):
        return pltpu.make_async_remote_copy(
            src_ref=zsend.at[c, zz],
            dst_ref=spec.at[c, z],
            send_sem=zsend_sem.at[c, zz],
            recv_sem=zrecv_sem.at[c, z],
            device_id=column_peer(zz),
            device_id_type=MESH,
        )

    def z_arrival(c, zz):
        return pltpu.make_async_remote_copy(
            src_ref=spec.at[c, zz],
            dst_ref=spec.at[c, zz],
            send_sem=zsend_sem.at[c, zz],
            recv_sem=zrecv_sem.at[c, zz],
            device_id=column_peer(zz),
            device_id_type=MESH,
        )

    def partial(u):
        c, zz, slot = u // SLABS, step_slab(lax.rem(u, SLABS)), lax.rem(u, LAG + 1)
        y_local(c, zz).wait()

        @pl.loop(1, PEERS)
        def _(d):
            y_arrival(c, zz, lax.rem(me + d, PEERS)).wait_recv()

        acc = dot_nn(weights[0], rbuf[c, zz, 0])
        for src in range(1, PEERS):
            acc = acc + dot_nn(weights[src], rbuf[c, zz, src])
        acc = acc.reshape(WB, 32, LANES)
        hsend[c, zz, 2:4] = acc[0:2]
        hsend[c, zz, 0:2] = acc[6:8]
        own[slot] = acc[2:6]
        helpers(c, zz, act_send=lambda copy: copy.start())

    def finish(u):
        c, zz, slot = u // SLABS, step_slab(lax.rem(u, SLABS)), lax.rem(u, LAG + 1)

        def take(copy, i):
            copy.wait_recv()
            own[slot, i] = own[slot, i] + hrecv[c, zz, i]

        helpers(c, zz, act_take=take)
        total = own[slot].astype(jnp.bfloat16).reshape(OWN * 32, LANES)
        rows = dot_nn(order, total).astype(jnp.bfloat16)

        @pl.when(zz == z)
        def _():
            spec[c, z] = rows

        @pl.when(zz != z)
        def _():
            zsend[c, zz] = rows
            z_copy(c, zz).start()

    def pipeline(first, last):
        @pl.loop(first, last)
        def _(u):
            partial(u)

            @pl.when(u + AHEAD < UNITS)
            def _():
                y_start(u + AHEAD)

            @pl.when(u >= LAG)
            def _():
                finish(u - LAG)

    def gather(c):
        @pl.loop(1, SLABS)
        def _(d):
            z_arrival(c, lax.rem(z + d, SLABS)).wait_recv()

        for pair in range(NF // 2):
            stacked = spec[c, :, pl.ds(pair * 16, 16), :].reshape(128, LANES)
            placed = dot_nn(arrange, stacked).astype(jnp.bfloat16)
            sxy[2 * pair, c] = placed[0:64]
            sxy[2 * pair + 1, c] = placed[64:128]
            products = dot_nt(placed, placed)
            if c > 0:
                products = products + gacc[pair]
            if c < 2:
                gacc[pair] = products
            else:
                for h in range(2):
                    k = h * 64
                    xx = products[k : k + 32, k : k + 32]
                    yy = products[k + 32 : k + 64, k + 32 : k + 64]
                    xy = products[k : k + 32, k + 32 : k + 64]
                    yx = products[k + 32 : k + 64, k : k + 32]
                    both = jnp.where(on_or_above, xx + yy, xy - yx)
                    gsend[2 * pair + h] = jnp.concatenate(
                        [both[8 * q : 8 * q + 8] for q in range(4)], 1
                    )

    row32 = lax.broadcasted_iota(jnp.int32, (NB, NB), 0)
    col32 = lax.broadcasted_iota(jnp.int32, (NB, NB), 1)
    on_or_above = col32 >= row32

    pipeline(0, 15)
    gather(0)
    pipeline(15, 23)
    gather(1)
    pipeline(23, UNITS)

    @pl.loop(UNITS - LAG, UNITS)
    def _(u):
        finish(u)

    gather(2)

    def g_copy(k):
        return pltpu.make_async_remote_copy(
            src_ref=gsend.at[k],
            dst_ref=grecv.at[plane_me],
            send_sem=gsend_sem.at[k],
            recv_sem=grecv_sem.at[plane_me],
            device_id=plane_peer(k),
            device_id_type=MESH,
        )

    def g_arrival(k):
        return pltpu.make_async_remote_copy(
            src_ref=grecv.at[k],
            dst_ref=grecv.at[k],
            send_sem=gsend_sem.at[k],
            recv_sem=grecv_sem.at[k],
            device_id=plane_peer(k),
            device_id_type=MESH,
        )

    def b_copy(k):
        return pltpu.make_async_remote_copy(
            src_ref=bsend,
            dst_ref=brecv.at[line_me],
            send_sem=bsend_sem.at[k],
            recv_sem=brecv_sem.at[line_me],
            device_id=line_peer(k),
            device_id_type=MESH,
        )

    def b_arrival(k):
        return pltpu.make_async_remote_copy(
            src_ref=brecv.at[k],
            dst_ref=brecv.at[k],
            send_sem=bsend_sem.at[k],
            recv_sem=brecv_sem.at[k],
            device_id=line_peer(k),
            device_id_type=MESH,
        )

    def c_copy(k):
        return pltpu.make_async_remote_copy(
            src_ref=csend,
            dst_ref=crecv.at[plane_me],
            send_sem=csend_sem.at[k],
            recv_sem=crecv_sem.at[plane_me],
            device_id=plane_peer(k),
            device_id_type=MESH,
        )

    def c_arrival(k):
        return pltpu.make_async_remote_copy(
            src_ref=crecv.at[k],
            dst_ref=crecv.at[k],
            send_sem=csend_sem.at[k],
            recv_sem=crecv_sem.at[k],
            device_id=plane_peer(k),
            device_id_type=MESH,
        )

    def others(mine, act):
        @pl.loop(1, 16)
        def _(d):
            act(lax.rem(mine + d, 16))

    others(plane_me, lambda k: g_copy(k).start())
    grecv[plane_me] = gsend[plane_me]

    @pl.loop(0, UNITS)
    def _(u):
        c, zz = u // SLABS, lax.rem(u, SLABS)

        @pl.loop(1, PEERS)
        def _(d):
            y_copy(c, zz, lax.rem(me + d, PEERS)).wait_send()

    others(plane_me, lambda k: g_arrival(k).wait_recv())
    bsend[...] = jnp.sum(grecv[...], axis=0)

    others(line_me, lambda k: b_copy(k).start())
    brecv[line_me] = bsend[...]

    @pl.loop(0, UNITS)
    def _(u):
        c, zz = u // SLABS, lax.rem(u, SLABS)
        helpers(c, zz, act_send=lambda copy: copy.wait_send())

        @pl.when(zz != z)
        def _():
            z_copy(c, zz).wait_send()

    others(plane_me, lambda k: g_copy(k).wait_send())
    others(line_me, lambda k: b_arrival(k).wait_recv())

    packed = jnp.sum(brecv[...], axis=0)
    both = jnp.concatenate([packed[:, 32 * k : 32 * k + 32] for k in range(4)], 0)
    flipped = both.T
    gram_re = jnp.where(on_or_above, both, flipped)
    gram_im = jnp.where(col32 < row32, both, jnp.where(col32 == row32, 0.0, -flipped))
    hermit = jnp.concatenate(
        [jnp.concatenate([gram_re, -gram_im], 1), jnp.concatenate([gram_im, gram_re], 1)], 0
    )
    row64 = lax.broadcasted_iota(jnp.int32, (64, 64), 0)
    eye = jnp.where(row64 == lax.broadcasted_iota(jnp.int32, (64, 64), 1), 1.0, 0.0)
    square = jnp.sum(jnp.sum(hermit * hermit, axis=1, keepdims=True), axis=0, keepdims=True)
    frob = jnp.sqrt(square + 1e-06)
    trace = jnp.sum(
        jnp.sum(jnp.where(col32 == row32, both, 0.0), axis=1, keepdims=True), axis=0, keepdims=True
    )
    iterate = hermit / frob
    high = lax.Precision.HIGHEST
    factor = 1.5 * eye - 0.5 * iterate
    inverse = factor
    iterate = dot_nn(iterate, factor, high)
    for iteration in range(1, NSIT):
        factor = 1.5 * eye - 0.5 * dot_nn(inverse, iterate, high)
        inverse = dot_nn(factor, inverse, high)
        if iteration < NSIT - 1:
            iterate = dot_nn(iterate, factor, high)
    columns = inverse[:, :NB] * jnp.sqrt(6.0 * POINTS / frob)
    energy = jnp.broadcast_to(trace / (3.0 * NB * POINTS), (16, LANES))
    high_part = energy.astype(jnp.bfloat16).astype(jnp.float32)
    mid_part = (energy - high_part).astype(jnp.bfloat16).astype(jnp.float32)
    low_part = energy - high_part - mid_part
    row16 = lax.broadcasted_iota(jnp.int32, (16, LANES), 0)
    parts = jnp.where(
        row16 == 0, high_part, jnp.where(row16 == 1, mid_part, jnp.where(row16 == 2, low_part, 0.0))
    )
    csend[0:16, :] = jnp.concatenate(
        [columns[16 * q : 16 * q + 16] for q in range(4)], 1
    ).astype(jnp.bfloat16)
    csend[16:32, :] = parts.astype(jnp.bfloat16)

    others(plane_me, lambda k: c_copy(k).start())
    crecv[plane_me] = csend[...]

    others(line_me, lambda k: b_copy(k).wait_send())
    others(plane_me, lambda k: c_copy(k).wait_send())
    others(plane_me, lambda k: c_arrival(k).wait_recv())
    coef_out[...] = crecv[...]


def combine(coefficients, spectra, modes, energy):
    pick_row = one_hot_rows(192, 64, lambda i: lax.rem(i, 2) * 32 + i // 6)
    row_c = lax.rem(lax.broadcasted_iota(jnp.int32, (192, 192), 0) // 2, 3)
    col_c = lax.broadcasted_iota(jnp.int32, (192, 192), 1) // 64
    same_c = row_c == col_c
    for f in range(STEP):
        message = coefficients[f]
        upper = jnp.concatenate([message[0:16, 0:32], message[0:16, 32:64]], 0)
        lower = jnp.concatenate([message[0:16, 64:96], message[0:16, 96:128]], 0)
        coef = jnp.concatenate(
            [jnp.concatenate([upper, lower], 1), jnp.concatenate([-lower, upper], 1)], 0
        )
        wide = dot_nt(pick_row, coef)
        wide = jnp.where(same_c, jnp.concatenate([wide, wide, wide], 1), 0.0).astype(jnp.bfloat16)
        stacked = spectra[f].reshape(192, LANES)
        modes[f * 192 : (f + 1) * 192, :] = dot_nn(wide, stacked).astype(jnp.bfloat16)
        parts = message[16:32].astype(jnp.float32)
        energy[pl.program_id(0) * STEP + f] = jnp.sum(parts[:, 0:1])


def local(snapshots, block_starts, freq_index):
    xt = jnp.transpose(snapshots, (1, 0, 2))
    dma = pltpu.SemaphoreType.DMA
    vmem = pltpu.VMEM
    bf, f32 = jnp.bfloat16, jnp.float32
    spectra, coefficients = pl.pallas_call(
        kernel,
        out_shape=(
            jax.ShapeDtypeStruct((NF, 3, 64, LANES), bf),
            jax.ShapeDtypeStruct((NF, 32, LANES), bf),
        ),
        in_specs=[
            pl.BlockSpec(memory_space=pl.ANY),
            pl.BlockSpec(memory_space=pltpu.HBM),
            pl.BlockSpec(memory_space=pltpu.HBM),
        ],
        out_specs=(
            pl.BlockSpec(memory_space=pltpu.VMEM),
            pl.BlockSpec(memory_space=pltpu.VMEM),
        ),
        scratch_shapes=[
            pltpu.SMEM((NB,), jnp.int32),
            pltpu.SMEM((NF,), jnp.int32),
            vmem((PEERS, WB * 32, ROWS), bf),
            vmem((3, SLABS, PEERS, ROWS, LANES), bf),
            vmem((LAG + 1, OWN, 32, LANES), f32),
            vmem((3, SLABS, 4, 32, LANES), f32),
            vmem((3, SLABS, 4, 32, LANES), f32),
            vmem((3, SLABS, 128, LANES), bf),
            vmem((3, SLABS, 128, LANES), bf),
            vmem((NF // 2, 128, LANES), f32),
            vmem((NF, 8, LANES), f32),
            vmem((NF, 8, LANES), f32),
            vmem((8, LANES), f32),
            vmem((16, 8, LANES), f32),
            vmem((32, LANES), bf),
            vmem((16, 32, LANES), bf),
            dma((3, SLABS, PEERS)),
            dma((3, SLABS, PEERS)),
            dma((3, SLABS, 4)),
            dma((3, SLABS, 4)),
            dma((3, SLABS)),
            dma((3, SLABS)),
            dma((16,)),
            dma((16,)),
            dma((16,)),
            dma((16,)),
            dma((16,)),
            dma((16,)),
            dma((2,)),
        ],
        compiler_params=pltpu.CompilerParams(
            collective_id=0, has_side_effects=True, vmem_limit_bytes=50 * 2**20
        ),
        name="spectra",
    )(xt, block_starts, freq_index)
    modes, energy = pl.pallas_call(
        combine,
        grid=(NF // STEP,),
        out_shape=(
            jax.ShapeDtypeStruct((NF * 192, LANES), bf),
            jax.ShapeDtypeStruct((NF,), f32),
        ),
        in_specs=[
            pl.BlockSpec((STEP, 32, LANES), lambda i: (i, 0, 0)),
            pl.BlockSpec((STEP, 3, 64, LANES), lambda i: (i, 0, 0, 0)),
        ],
        out_specs=(
            pl.BlockSpec((STEP * 192, LANES), lambda i: (i, 0)),
            pl.BlockSpec(memory_space=pltpu.SMEM),
        ),
        compiler_params=pltpu.CompilerParams(vmem_limit_bytes=50 * 2**20),
        name="modes",
    )(coefficients, spectra)
    modes = modes.reshape(NF, NB, 3, 2, LANES)
    return (jnp.transpose(modes, (0, 1, 3, 2, 4)), energy)


def solution(mesh):
    return jax.shard_map(
        local,
        mesh=mesh,
        in_specs=(P("tm", None, "freq"), P(), P()),
        out_specs=(P(None, None, None, None, ("freq", "tm")), P()),
        check_vma=False,
    )
```

time: 106 us -> 89.5 us (0.84)
  Pallas kernels: 98.6 us -> 87.4 us
  local copies, waits for them, and re-layouts: 4.55 us -> 1.3 us
  other arithmetic: 1.51 us -> 0 us
    pallas_call x1 -> x2, Pallas kernels: 98.6 us -> 87.4 us  [the longest x1 84 us: local(): pl.pallas_call(kernel, out_shape=(jax.ShapeDtypeStruct((NF, 3, 64, LANES)...]
    slice x1 -> x0, local copies, waits for them, and re-layouts: 1.32 us -> none  [local(): return (jnp.transpose(modes, (0, 1, 3, 2, 4)), energy[:, 0])]
    unnamed x1 -> x4, local copies, waits for them, and re-layouts: 2.59 us -> 1.3 us
where the time goes in v2:
time: 89.5 us; the launch traced here: 89.4 us
  Pallas kernels  87.4 us (98%)
  local copies, waits for them, and re-layouts  1.3 us (1%)
    pallas_call x1, Pallas kernels, local(): pl.pallas_call(kernel, out_shape=(jax.ShapeDtypeStruct((NF, 3, 64, LANES)...  84 us
    pallas_call x1, Pallas kernels, local(): pl.pallas_call(combine, grid=(NF // STEP,), out_shape=(jax.ShapeDtypeStru...  3.42 us

profile of v2, /device:TPU:1, one launch (start us, length us, event | category | flops | bytes accessed | tf_op | source)
XLA Modules:
  0.0 89.4 jit_solution(4614547159888531442)
XLA Ops:
  0.6 0.0 copy-start
  0.6 0.6 copy-done
  1.3 0.0 copy-start.1
  1.3 0.7 copy-done.1
  1.9 84.0 %spectra.1 = (bf16[16,3,64,128]{3,2,1,0:T(8,128)(2,1)S(1)}, bf16[16,32,128]{2,1,0:T(8,128)(2,1)S(1)}) custom-call(bf16[3,68,8192]{2,1,0:T(8,128)(2,1)} %bitcast.4, s32[32]{0:T(128)S(1)} %copy-done, s32[16]{0:T(128)S(1)} %copy-done.1), custom_call_target="tpu_custom_call" | custom-call | tf_op jit(solution)/shard_map/spectra/pallas_call | solution.py:519
  86.0 3.4 %modes.1 = (bf16[3072,128]{1,0:T(8,128)(2,1)}, f32[16]{0:T(128)}) custom-call(bf16[16,32,128]{2,1,0:T(8,128)(2,1)S(1)} %get-tuple-element.6.coefficients, bf16[16,3,64,128]{3,2,1,0:T(8,128)(2,1)S(1)} %get-tuple-element.7.spectra), custom_call_target="tpu_custom_call" | custom-call | tf_op jit(solution)/shard_map/modes/pallas_call | solution.py:570
Async XLA Ops:
  0.6 0.7 copy-start
  1.3 0.7 copy-start.1

commit v3 on v2

--- a/solution.py
+++ b/solution.py
@@ -20,18 +20,21 @@
 UNITS = 3 * SLABS
 AHEAD = 6
 LAG = 3
+HOPS = 4
+MAIN = 64
+REST = 4
 STEP = 16
 LANES = 128
 POINTS = 32768.0
 MESH = pl.DeviceIdType.MESH
 
 
-def dft_rows(freq):
+def dft_rows(small):
     row = lax.broadcasted_iota(jnp.int32, (2 * NF, NFFT), 0)
     time = lax.broadcasted_iota(jnp.int32, (2 * NF, NFFT), 1)
     bins = jnp.zeros((2 * NF, NFFT), jnp.int32)
     for f in range(NF):
-        bins = jnp.where(row // 2 == f, freq[f], bins)
+        bins = jnp.where(row // 2 == f, small[NB + f], bins)
     angles = 2.0 * math.pi / NFFT * lax.rem(bins * time, NFFT).astype(jnp.float32)
     window = 0.5 - 0.5 * jnp.cos(2.0 * math.pi / NFFT * time[0:8].astype(jnp.float32))
     scaling = 1.0 / jnp.sqrt(jnp.sum((window * window)[0:1], axis=1, keepdims=True))
@@ -64,13 +67,15 @@
 
 def kernel(
     xt,
-    starts_hbm,
-    freq_hbm,
+    small_hbm,
     sxy,
     coef_out,
-    starts,
-    freq,
+    small,
     weights,
+    rest_weights,
+    rest_stage,
+    rest_send,
+    rest_recv,
     rbuf,
     own,
     hsend,
@@ -97,6 +102,9 @@
     csend_sem,
     crecv_sem,
     small_sem,
+    news_sem,
+    rest_send_sem,
+    rest_recv_sem,
 ):
     tm = lax.axis_index("tm")
     fx = lax.axis_index("freq")
@@ -120,12 +128,17 @@
     plane_me = fx * 4 + y
     line_me = z * 2 + core
 
-    starts_copy = pltpu.make_async_copy(starts_hbm, starts, small_sem.at[0])
-    freq_copy = pltpu.make_async_copy(freq_hbm, freq, small_sem.at[1])
-    starts_copy.start()
-    freq_copy.start()
+    small_copy = pltpu.make_async_copy(small_hbm, small, small_sem.at[0])
+    rest_copy = pltpu.make_async_copy(xt.at[:, pl.ds(MAIN, REST), :], rest_stage, small_sem.at[1])
+    rest_copy.start()
+    small_copy.start()
 
     barrier = pltpu.get_barrier_semaphore()
+
+    def around(k):
+        zs = lax.rem(z + (SLABS + 1, SLABS - 1, SLABS, SLABS)[k], SLABS)
+        xs = lax.rem(fx + (4, 4, 5, 3)[k], 4)
+        return {"tm": zs * PEERS + me, "freq": xs}
 
     def greet(device):
         pl.semaphore_signal(barrier, inc=1, device_id=device, device_id_type=MESH)
@@ -134,21 +147,55 @@
     def _(d):
         greet(slab_peer(lax.rem(me + d, PEERS)))
 
-    @pl.loop(1, 16)
+    for k in range(4):
+        greet(around(k))
+
+    def tell(hop):
+        for k in range(4):
+            pl.semaphore_signal(
+                news_sem.at[hop, k], inc=1, device_id=around(k), device_id_type=MESH
+            )
+
+    def hear(hop):
+        for k in range(4):
+            pl.semaphore_wait(news_sem.at[hop, k], 1)
+
+    small_copy.wait()
+    table = dft_rows(small)
+    rest_copy.wait()
+    for c in range(3):
+        for zz in range(SLABS):
+            for p in range(PEERS):
+                col = (zz * PEERS + p) * LANES
+                rest_send[p, c, zz * REST : zz * REST + REST, :] = rest_stage[
+                    c, :, col : col + LANES
+                ]
+
+    pl.semaphore_wait(barrier, 11)
+    tell(0)
+
+    def seat(p):
+        return pl.ds(pl.multiple_of(p * MAIN, MAIN), MAIN)
+
+    def rest_move(p, source):
+        return pltpu.make_async_remote_copy(
+            src_ref=rest_send.at[p],
+            dst_ref=rest_recv.at[source],
+            send_sem=rest_send_sem.at[p],
+            recv_sem=rest_recv_sem.at[source],
+            device_id=slab_peer(p),
+            device_id_type=MESH,
+        )
+
+    @pl.loop(1, PEERS)
     def _(d):
-        greet(plane_peer(lax.rem(plane_me + d, 16)))
-        greet(line_peer(lax.rem(line_me + d, 16)))
-
-    starts_copy.wait()
-    freq_copy.wait()
-    table = dft_rows(freq)
-    pl.semaphore_wait(barrier, 37)
+        rest_move(lax.rem(me + d, PEERS), me).start()
 
     def y_copy(c, zz, p):
         cols = pl.ds(pl.multiple_of((zz * PEERS + p) * LANES, LANES), LANES)
         return pltpu.make_async_remote_copy(
-            src_ref=xt.at[c, :, cols],
-            dst_ref=rbuf.at[c, zz, me],
+            src_ref=xt.at[c, pl.ds(0, MAIN), cols],
+            dst_ref=rbuf.at[c, zz, seat(me)],
             send_sem=ysend_sem.at[c, zz, p],
             recv_sem=yrecv_sem.at[c, zz, me],
             device_id=slab_peer(p),
@@ -157,8 +204,8 @@
 
     def y_arrival(c, zz, p):
         return pltpu.make_async_remote_copy(
-            src_ref=rbuf.at[c, zz, p],
-            dst_ref=rbuf.at[c, zz, p],
+            src_ref=rbuf.at[c, zz, seat(p)],
+            dst_ref=rbuf.at[c, zz, seat(p)],
             send_sem=ysend_sem.at[c, zz, p],
             recv_sem=yrecv_sem.at[c, zz, p],
             device_id=slab_peer(p),
@@ -168,7 +215,7 @@
     def y_local(c, zz):
         cols = pl.ds(pl.multiple_of((zz * PEERS + me) * LANES, LANES), LANES)
         return pltpu.make_async_copy(
-            xt.at[c, :, cols], rbuf.at[c, zz, me], yrecv_sem.at[c, zz, me]
+            xt.at[c, pl.ds(0, MAIN), cols], rbuf.at[c, zz, seat(me)], yrecv_sem.at[c, zz, me]
         )
 
     def y_start(u):
@@ -184,16 +231,30 @@
     def _(u):
         y_start(u)
 
-    tau = lax.broadcasted_iota(jnp.int32, (NFFT, ROWS), 0)
-    tt = lax.broadcasted_iota(jnp.int32, (NFFT, ROWS), 1)
-    lag = tau - tt
+    tau = lax.broadcasted_iota(jnp.int32, (NFFT, LANES), 0)
+    lane = lax.broadcasted_iota(jnp.int32, (NFFT, LANES), 1)
+    lag = tau - (lane // MAIN * ROWS + lax.rem(lane, MAIN))
+    rest_lag = tau - (lane // 32 * ROWS + MAIN + lax.rem(lane, REST))
+
+    def placed_rows(lags, value):
+        pick = jnp.where(lags == value, 1.0, 0.0).astype(jnp.bfloat16)
+        return dot_nn(table, pick).astype(jnp.bfloat16)
+
     for i in range(WB):
         b = z * OWN - 2 + i
-        first = starts[jnp.clip(b, 0, NB - 1)]
-        for src in range(PEERS):
-            origin = z * (PEERS * ROWS) + src * ROWS
-            pick = jnp.where(lag == origin - first, 1.0, 0.0).astype(jnp.bfloat16)
-            weights[src, pl.ds(i * 32, 32), :] = dot_nn(table, pick).astype(jnp.bfloat16)
+        late = z * (PEERS * ROWS) - small[jnp.clip(b, 0, NB - 1)]
+        rows = slice(i * 32, i * 32 + 32)
+        for q in range(4):
+            weights[rows, q * LANES : (q + 1) * LANES] = placed_rows(lag, late + 2 * q * ROWS)
+        for q in range(2):
+            rest_weights[rows, q * LANES : (q + 1) * LANES] = placed_rows(
+                rest_lag, late + 4 * q * ROWS
+            )
+
+    for hop in range(HOPS - 1):
+        hear(hop)
+        tell(hop + 1)
+    hear(HOPS - 1)
 
     order = one_hot_rows(128, 128, lambda i: lax.rem(i // 2, 4) * 32 + (i // 8) * 2 + lax.rem(i, 2))
     arrange = one_hot_rows(
@@ -256,6 +317,8 @@
             device_id_type=MESH,
         )
 
+    rest_lane = lax.broadcasted_iota(jnp.int32, (WB * 32, PEERS * 32), 1)
+
     def partial(u):
         c, zz, slot = u // SLABS, step_slab(lax.rem(u, SLABS)), lax.rem(u, LAG + 1)
         y_local(c, zz).wait()
@@ -264,9 +327,10 @@
         def _(d):
             y_arrival(c, zz, lax.rem(me + d, PEERS)).wait_recv()
 
-        acc = dot_nn(weights[0], rbuf[c, zz, 0])
-        for src in range(1, PEERS):
-            acc = acc + dot_nn(weights[src], rbuf[c, zz, src])
+        mine = lax.rem(rest_lane // REST, SLABS) == zz
+        chosen = jnp.where(mine, rest_weights[...].astype(jnp.float32), 0.0).astype(jnp.bfloat16)
+        acc = dot_nn(weights[...], rbuf[c, zz])
+        acc = acc + dot_nn(chosen, rest_recv[:, c].reshape(PEERS * 32, LANES))
         acc = acc.reshape(WB, 32, LANES)
         hsend[c, zz, 2:4] = acc[0:2]
         hsend[c, zz, 0:2] = acc[6:8]
@@ -336,6 +400,14 @@
     row32 = lax.broadcasted_iota(jnp.int32, (NB, NB), 0)
     col32 = lax.broadcasted_iota(jnp.int32, (NB, NB), 1)
     on_or_above = col32 >= row32
+
+    rest_recv[me] = rest_send[me]
+
+    @pl.loop(1, PEERS)
+    def _(d):
+        p = lax.rem(me + d, PEERS)
+        rest_move(p, p).wait_recv()
+        rest_move(p, p).wait_send()
 
     pipeline(0, 15)
     gather(0)
@@ -525,17 +597,19 @@
         in_specs=[
             pl.BlockSpec(memory_space=pl.ANY),
             pl.BlockSpec(memory_space=pltpu.HBM),
-            pl.BlockSpec(memory_space=pltpu.HBM),
         ],
         out_specs=(
             pl.BlockSpec(memory_space=pltpu.VMEM),
             pl.BlockSpec(memory_space=pltpu.VMEM),
         ),
         scratch_shapes=[
-            pltpu.SMEM((NB,), jnp.int32),
-            pltpu.SMEM((NF,), jnp.int32),
-            vmem((PEERS, WB * 32, ROWS), bf),
-            vmem((3, SLABS, PEERS, ROWS, LANES), bf),
+            pltpu.SMEM((NB + NF,), jnp.int32),
+            vmem((WB * 32, PEERS * MAIN), bf),
+            vmem((WB * 32, PEERS * 32), bf),
+            vmem((3, REST, SLABS * PEERS * LANES), bf),
+            vmem((PEERS, 3, 32, LANES), bf),
+            vmem((PEERS, 3, 32, LANES), bf),
+            vmem((3, SLABS, PEERS * MAIN, LANES), bf),
             vmem((LAG + 1, OWN, 32, LANES), f32),
             vmem((3, SLABS, 4, 32, LANES), f32),
             vmem((3, SLABS, 4, 32, LANES), f32),
@@ -561,12 +635,15 @@
             dma((16,)),
             dma((16,)),
             dma((2,)),
+            pltpu.SemaphoreType.REGULAR((HOPS, 4)),
+            dma((PEERS,)),
+            dma((PEERS,)),
         ],
         compiler_params=pltpu.CompilerParams(
             collective_id=0, has_side_effects=True, vmem_limit_bytes=50 * 2**20
         ),
         name="spectra",
-    )(xt, block_starts, freq_index)
+    )(xt, jnp.concatenate([block_starts, freq_index]))
     modes, energy = pl.pallas_call(
         combine,
         grid=(NF // STEP,),

time: 89.5 us -> 86.5 us (0.966)
  Pallas kernels: 87.4 us -> 85 us
  local copies, waits for them, and re-layouts: 1.3 us -> 0 us
    pallas_call x1, Pallas kernels: 84 us -> 81.6 us  [local(): pl.pallas_call(kernel, out_shape=(jax.ShapeDtypeStruct((NF, 3, 64, LANES)...]
    unnamed x4 -> x0, local copies, waits for them, and re-layouts: 1.3 us -> none
where the time goes in v3:
time: 86.5 us; the launch traced here: 86.4 us
  Pallas kernels  85 us (98%)
    pallas_call x1, Pallas kernels, local(): pl.pallas_call(kernel, out_shape=(jax.ShapeDtypeStruct((NF, 3, 64, LANES)...  81.6 us
    pallas_call x1, Pallas kernels, local(): pl.pallas_call(combine, grid=(NF // STEP,), out_shape=(jax.ShapeDtypeStru...  3.42 us

profile of v3, /device:TPU:1, one launch (start us, length us, event | category | flops | bytes accessed | tf_op | source)
XLA Modules:
  0.0 86.4 jit_solution(10454774459439229465)
XLA Ops:
  0.6 0.7 pad_add_fusion.small_hbm
  1.4 81.6 %spectra.1 = (bf16[16,3,64,128]{3,2,1,0:T(8,128)(2,1)S(1)}, bf16[16,32,128]{2,1,0:T(8,128)(2,1)S(1)}) custom-call(bf16[3,68,8192]{2,1,0:T(8,128)(2,1)} %bitcast.4, s32[48]{0:T(128)S(1)} %pad_add_fusion.small_hbm), custom_call_target="tpu_custom_call" | custom-call | tf_op jit(solution)/shard_map/spectra/pallas_call | solution.py:591
  83.0 3.4 %modes.1 = (bf16[3072,128]{1,0:T(8,128)(2,1)}, f32[16]{0:T(128)}) custom-call(bf16[16,32,128]{2,1,0:T(8,128)(2,1)S(1)} %get-tuple-element.6.coefficients, bf16[16,3,64,128]{3,2,1,0:T(8,128)(2,1)S(1)} %get-tuple-element.7.spectra), custom_call_target="tpu_custom_call" | custom-call | tf_op jit(solution)/shard_map/modes/pallas_call | solution.py:647

commit v4 on v3

--- a/solution.py
+++ b/solution.py
@@ -575,8 +575,8 @@
         coef = jnp.concatenate(
             [jnp.concatenate([upper, lower], 1), jnp.concatenate([-lower, upper], 1)], 0
         )
-        wide = dot_nt(pick_row, coef)
-        wide = jnp.where(same_c, jnp.concatenate([wide, wide, wide], 1), 0.0).astype(jnp.bfloat16)
+        wide = dot_nt(pick_row, jnp.concatenate([coef, coef, coef], 0))
+        wide = jnp.where(same_c, wide, 0.0).astype(jnp.bfloat16)
         stacked = spectra[f].reshape(192, LANES)
         modes[f * 192 : (f + 1) * 192, :] = dot_nn(wide, stacked).astype(jnp.bfloat16)
         parts = message[16:32].astype(jnp.float32)

time: 86.5 us -> 85.6 us (0.990)
  Pallas kernels: 85 us -> 84.1 us
    pallas_call x1, Pallas kernels: 3.42 us -> 2.46 us  [local(): pl.pallas_call(combine, grid=(NF // STEP,), out_shape=(jax.ShapeDtypeStru...]
where the time goes in v4:
time: 85.6 us; the launch traced here: 85.4 us
  Pallas kernels  84.1 us (98%)
    pallas_call x1, Pallas kernels, local(): pl.pallas_call(kernel, out_shape=(jax.ShapeDtypeStruct((NF, 3, 64, LANES)...  81.6 us
    pallas_call x1, Pallas kernels, local(): pl.pallas_call(combine, grid=(NF // STEP,), out_shape=(jax.ShapeDtypeStru...  2.46 us

profile of v4, /device:TPU:1, one launch (start us, length us, event | category | flops | bytes accessed | tf_op | source)
XLA Modules:
  0.0 85.4 jit_solution(13855545739725295814)
XLA Ops:
  0.6 0.7 pad_add_fusion.small_hbm
  1.4 81.6 %spectra.1 = (bf16[16,3,64,128]{3,2,1,0:T(8,128)(2,1)S(1)}, bf16[16,32,128]{2,1,0:T(8,128)(2,1)S(1)}) custom-call(bf16[3,68,8192]{2,1,0:T(8,128)(2,1)} %bitcast.4, s32[48]{0:T(128)S(1)} %pad_add_fusion.small_hbm), custom_call_target="tpu_custom_call" | custom-call | tf_op jit(solution)/shard_map/spectra/pallas_call | solution.py:591
  83.0 2.5 %modes.1 = (bf16[3072,128]{1,0:T(8,128)(2,1)}, f32[16]{0:T(128)}) custom-call(bf16[16,32,128]{2,1,0:T(8,128)(2,1)S(1)} %get-tuple-element.6.coefficients, bf16[16,3,64,128]{3,2,1,0:T(8,128)(2,1)S(1)} %get-tuple-element.7.spectra), custom_call_target="tpu_custom_call" | custom-call | tf_op jit(solution)/shard_map/modes/pallas_call | solution.py:647
